TPU v7x, 32 devices: a whole 2x2x4 slice. The times are simulated.
32 devices in a mesh: block: 4 (over y, x), span: 4 (over z), heads: 2 (over core).
Axes of the slice: x: 2, y: 2, z: 4, core: 2. Of those that a mesh axis runs over, the one named last changes fastest.
Arguments:
- fresh_keys: bfloat16 [16, 8192, 8, 128], P(None, ('block', 'span'), 'heads'), may hold values from -6 to 6
- fresh_values: bfloat16 [16, 8192, 8, 128], P(None, ('block', 'span'), 'heads'), may hold values from -6 to 6
- turn_angle: float32 [8192, 64], replicated, may hold values from -3.140625 to 3.140625
Outputs:
- stored_keys: bfloat16 [16, 8192, 8, 128], P(('block', 'span'), None, 'heads')
- stored_values: bfloat16 [16, 8192, 8, 128], P(('block', 'span'), None, 'heads')
- key_scale: float32 [16, 8, 128], P(('block', 'span'), 'heads')
All inputs are finite; a program needn't handle non-finite values. Where the computation divides by a largest or mean magnitude, that divisor is 1e-20 or more.
Results may differ from a plain program's by a relative error of at most 0.001.
Values may be sent and summed in bfloat16 or wider, within the bound.
A program may use at most 192 MiB of HBM per device.

v0:
```python
import jax
import jax.numpy as jnp
from jax import lax
from jax.sharding import PartitionSpec as P


def rotate_pairs(vectors, angle):
    half = vectors.shape[-1] // 2
    cosine, sine = (jnp.cos(angle)[None, :, None, :], jnp.sin(angle)[None, :, None, :])
    first, second = (vectors[..., :half], vectors[..., half:])
    return jnp.concatenate(
        [first * cosine - second * sine, second * cosine + first * sine], axis=-1
    )


def keys_in_place(plain_keys, angle):
    wide_keys = plain_keys.astype(jnp.float32)
    return rotate_pairs(wide_keys, angle)


def local(fresh_keys, fresh_values, turn_angle):
    moved_keys, stored_values = (
        lax.all_to_all(fresh_keys, ("block", "span"), split_axis=0, concat_axis=1, tiled=True),
        lax.all_to_all(fresh_values, ("block", "span"), split_axis=0, concat_axis=1, tiled=True),
    )
    turned_keys = keys_in_place(moved_keys, turn_angle)
    key_scale = jnp.max(jnp.abs(turned_keys), axis=1)
    narrow_keys = (turned_keys / key_scale[:, None]).astype(jnp.bfloat16)
    return (narrow_keys, stored_values, key_scale)


def solution(mesh):
    return jax.shard_map(
        local,
        mesh=mesh,
        in_specs=(
            P(None, ("block", "span"), "heads", None),
            P(None, ("block", "span"), "heads", None),
            P(),
        ),
        out_specs=(
            P(("block", "span"), None, "heads", None),
            P(("block", "span"), None, "heads", None),
            P(("block", "span"), "heads", None),
        ),
        check_vma=False,
    )
```

profile of v0, /device:TPU:0, one launch (start us, length us, event | category | flops | bytes accessed | tf_op | source)
XLA Modules:
  0.0 407.9 jit_solution(4668758468986669054)
XLA Ops:
  0.6 193.2 %all_to_all.21 = bf16[16,512,4,128]{3,2,1,0:T(4,128)(2,1)} all-to-all(bf16[16,512,4,128]{3,2,1,0:T(4,128)(2,1)} %param.3), channel_id=1, replica_groups=mesh['block'=4,'span'=4,'heads'=2] {'block','span'}, dimensions={0} | all-to-all | bytes 16777216 | tf_op jit(solution)/shard_map/all_to_all | solution.py:23
  193.8 4.8 %all-to-all-start.1 = ((bf16[16,512,4,128]{3,2,1,0:T(4,128)(2,1)}), bf16[16,512,4,128]{3,2,1,0:T(4,128)(2,1)}, u32[]{:S(2)}, u32[]{:S(2)}) async-start(bf16[16,512,4,128]{3,2,1,0:T(4,128)(2,1)} %param.4), calls=%async_computation.1 | async-start | bytes 16777216 | tf_op jit(solution)/shard_map/all_to_all | solution.py:24
  198.6 9.4 %fusion = (f32[8192,64]{0,1:T(8,128)}, f32[8192,64]{0,1:T(8,128)S(1)}) fusion(f32[8192,64]{0,1:T(8,128)} %param.5), kind=kLoop, calls=%fused_computation.6 | loop fusion | bytes 6291456 | tf_op jit(solution)/shard_map/cos | solution.py:9
  208.0 3.8 copy.6
  211.8 2.8 copy.7
  214.6 0.0 copy-start.2
  214.6 0.0 copy-start.3
  214.6 5.9 %bitcast_convert_fusion = f32[1,4096,8,128]{3,2,1,0:T(8,128)S(1)} fusion(bf16[1,4096,8,128]{3,2,1,0:T(8,128)(2,1)} %bitcast.9), kind=kLoop, calls=%fused_computation.5 | loop fusion | flops 4194304 | bytes 25165824 | tf_op jit(solution)/shard_map/convert_element_type | solution.py:17
  220.5 0.0 copy-done.2
  220.5 0.1 copy-done.3
  220.6 14.5 %multiply_subtract_fusion = (f32[1,8192,4,64]{3,2,1,0:T(4,128)}, f32[1,8192,4,64]{3,2,1,0:T(4,128)}) fusion(f32[1,8192,4,128]{3,2,1,0:T(4,128)S(1)} %bitcast.8, f32[8192,64]{1,0:T(8,128)S(1)} %copy-done.3, f32[8192,64]{1,0:T(8,128)S(1)} %copy-done.2), kind=kLoop, calls=%fused_computation.3 | loop fusion | flops 12582912 | bytes 37748736 | tf_op jit(solution)/shard_map/sub | solution.py:12
  235.0 0.0 copy-start
  235.0 0.0 copy-start.1
  235.0 19.4 %abs_reduce_fusion = f32[4,128]{1,0:T(4,128)S(1)} fusion(f32[1,8192,4,64]{3,2,1,0:T(4,128)} %get-tuple-element.4, f32[1,8192,4,64]{3,2,1,0:T(4,128)} %get-tuple-element.3), kind=kLoop, calls=%fused_computation.1 | loop fusion | flops 12582400 | bytes 16779264 | tf_op jit(solution)/shard_map/reduce_max | solution.py:27
  254.4 0.0 copy-done
  254.5 1.0 copy-done.1
  255.4 0.0 copy-start.4
  255.4 10.3 %divide_convert_fusion = bf16[1,8192,4,128]{3,2,1,0:T(4,128)(2,1)} fusion(f32[4,128]{1,0:T(4,128)S(1)} %abs_reduce_fusion, f32[1,8192,4,64]{3,2,1,0:T(4,128)S(1)} %copy-done.1, f32[1,8192,4,64]{3,2,1,0:T(4,128)S(1)} %copy-done), kind=kLoop, calls=%fused_computation.4 | loop fusion | flops 12582912 | bytes 25167872 | tf_op jit(solution)/shard_map/convert_element_type | solution.py:28
  265.7 0.0 copy-done.4
  265.7 134.2 %all-to-all-done.1 = bf16[16,512,4,128]{3,2,1,0:T(4,128)(2,1)} async-done(((bf16[16,512,4,128]{3,2,1,0:T(4,128)(2,1)}), bf16[16,512,4,128]{3,2,1,0:T(4,128)(2,1)}, u32[]{:S(2)}, u32[]{:S(2)}) %all-to-all-start.1) | async-done | bytes 8388640 | tf_op jit(solution)/shard_map/all_to_all | solution.py:24
  399.9 8.1 %copy.9 = bf16[1,8192,4,128]{3,2,1,0:T(4,128)(2,1)} copy(bf16[1,8192,4,128]{3,2,1,0:T(4,128)(2,1)} %bitcast.2) | data formatting | bytes 16777216
Async XLA Ops:
  193.8 206.0 %all-to-all-start.1 = ((bf16[16,512,4,128]{3,2,1,0:T(4,128)(2,1)}), bf16[16,512,4,128]{3,2,1,0:T(4,128)(2,1)}, u32[]{:S(2)}, u32[]{:S(2)}) async-start(bf16[16,512,4,128]{3,2,1,0:T(4,128)(2,1)} %param.4), calls=%async_computation.1 | async-start | bytes 16777216 | tf_op jit(solution)/shard_map/all_to_all | solution.py:24
  214.6 5.9 %copy-start.2 = (f32[8192,64]{1,0:T(8,128)S(1)}, f32[8192,64]{1,0:T(8,128)}, u32[]{:S(2)}) copy-start(f32[8192,64]{1,0:T(8,128)} %copy.6) | copy-start | bytes 6291460
  214.6 6.0 %copy-start.3 = (f32[8192,64]{1,0:T(8,128)S(1)}, f32[8192,64]{1,0:T(8,128)}, u32[]{:S(2)}) copy-start(f32[8192,64]{1,0:T(8,128)} %copy.7) | copy-start | bytes 6291460
  235.0 19.4 %copy-start = (f32[1,8192,4,64]{3,2,1,0:T(4,128)S(1)}, f32[1,8192,4,64]{3,2,1,0:T(4,128)}, u32[]{:S(2)}) copy-start(f32[1,8192,4,64]{3,2,1,0:T(4,128)} %get-tuple-element.3) | copy-start | bytes 25165828
  235.0 20.4 %copy-start.1 = (f32[1,8192,4,64]{3,2,1,0:T(4,128)S(1)}, f32[1,8192,4,64]{3,2,1,0:T(4,128)}, u32[]{:S(2)}) copy-start(f32[1,8192,4,64]{3,2,1,0:T(4,128)} %get-tuple-element.4) | copy-start | bytes 25165828
  255.4 10.3 %copy-start.4 = (f32[4,128]{1,0:T(4,128)}, f32[4,128]{1,0:T(4,128)S(1)}, u32[]{:S(2)}) copy-start(f32[4,128]{1,0:T(4,128)S(1)} %abs_reduce_fusion) | copy-start | bytes 6148
where the time goes:
time: 408 us
  blocking collectives  193 us (47%)
  waiting for transfers between devices  134 us (33%)
  other arithmetic  50 us (12%)
  local copies, waits for them, and re-layouts  25.1 us (6%)
  starting transfers between devices  4.75 us (1%)
    all_to_all x1, blocking collectives, local(): lax.all_to_all(fresh_keys, ('block', 'span'), split_axis=0, concat_axis=1...  193 us
    all_to_all x1, waiting for transfers between devices, local(): lax.all_to_all(fresh_values, ('block', 'span'), split_axis=0, concat_axis...  134 us
    reduce_max x1, other arithmetic, local(): key_scale = jnp.max(jnp.abs(turned_keys), axis=1)  19.4 us
    sub x1, other arithmetic, rotate_pairs(): first * cosine - second * sine  14.5 us
    cos x2, local copies, waits for them, and re-layouts, rotate_pairs(): jnp.cos(angle)[None, :, None, :]  13.3 us
    convert_element_type x1, other arithmetic, local(): narrow_keys = (turned_keys / key_scale[:, None]).astype(jnp.bfloat16)  10.3 us
    unnamed x11, local copies, waits for them, and re-layouts  9.08 us
  transfers between devices with their start and end apart: 1, of which 1 were waited for; matrix products, arithmetic and copies ran while one was open for 16% of the time, Pallas kernels for 0%

commit v1 on v0

v1 whole, which is shorter than its diff:
```python
import math

import jax
import jax.numpy as jnp
from jax import lax
from jax.experimental import pallas as pl
from jax.experimental.pallas import tpu as pltpu
from jax.sharding import PartitionSpec as P


HBM = pl.BlockSpec(memory_space=pltpu.HBM)


def rotate_pairs(vectors, angle):
    half = vectors.shape[-1] // 2
    cosine, sine = (jnp.cos(angle)[None, :, None, :], jnp.sin(angle)[None, :, None, :])
    first, second = (vectors[..., :half], vectors[..., half:])
    return jnp.concatenate(
        [first * cosine - second * sine, second * cosine + first * sine], axis=-1
    )


def carry(pairs, held, arrived, left):
    into = [pltpu.make_async_copy(a, held.at[i], arrived.at[i]) for i, (a, b) in enumerate(pairs)]
    away = [pltpu.make_async_copy(held.at[i], b, left.at[i]) for i, (a, b) in enumerate(pairs)]
    for copy in into:
        copy.start()
    for one, two in zip(into, away):
        one.wait()
        two.start()
    for copy in away:
        copy.wait()


def solution(mesh):
    axes = ("block", "span")
    n = mesh.shape["block"] * mesh.shape["span"]
    stride = next(k for k in range(min(7, n - 1), 0, -1) if math.gcd(k, n) == 1)
    steps = sorted(range(1, n), key=lambda d: (d * stride) % n)

    def peer(index, step, sign=1):
        return (index + n + sign * step) % n

    def params(count, x):
        rows = x.shape[0] // n
        size = count * rows * x.shape[1] * x.shape[2] * x.shape[3] * x.dtype.itemsize
        return dict(
            scratch_shapes=[
                pltpu.VMEM((count, rows) + x.shape[1:], x.dtype),
                pltpu.SemaphoreType.DMA((count,)),
                pltpu.SemaphoreType.DMA((count,)),
            ],
            compiler_params=pltpu.CompilerParams(vmem_limit_bytes=2 * size + 2**22),
            cost_estimate=pl.CostEstimate(flops=0, bytes_accessed=2 * size, transcendentals=0),
        )

    def cut(x, shifts, after):
        rows = x.shape[0] // n

        def kernel(x_ref, after_ref, *rest):
            outs, scratch = rest[: len(shifts)], rest[len(shifts) :]
            me = lax.axis_index(axes)
            carry(
                [(x_ref.at[pl.ds(peer(me, d) * rows, rows)], o) for d, o in zip(shifts, outs)],
                *scratch,
            )

        shape = jax.ShapeDtypeStruct((rows,) + x.shape[1:], x.dtype)
        return pl.pallas_call(
            kernel,
            out_shape=[shape] * len(shifts),
            in_specs=[HBM, HBM],
            out_specs=[HBM] * len(shifts),
            name="cut",
            **params(len(shifts), x),
        )(x, after)

    def shift(block, d):
        return lax.ppermute(block, axes, [(i, peer(i, d)) for i in range(n)])

    def join(x, shifts, blocks, whole, after):
        rows, piece = x.shape[0] // n, x.shape[1]

        def kernel(*refs):
            ins, out, scratch = refs[: len(shifts)], refs[-4], refs[-3:]
            me = lax.axis_index(axes)
            pairs = []
            for d, ref in zip(shifts, ins):
                at = peer(me, d, -1)
                source = ref if d else ref.at[pl.ds(me * rows, rows)]
                pairs.append((source, out.at[:, pl.ds(at * piece, piece)]))
            carry(pairs, *scratch)

        given = list(blocks) + [after] + ([] if whole is None else [whole])
        return pl.pallas_call(
            kernel,
            out_shape=jax.ShapeDtypeStruct((rows, n * piece) + x.shape[2:], x.dtype),
            in_specs=[HBM] * len(given),
            out_specs=HBM,
            input_output_aliases={} if whole is None else {len(given) - 1: 0},
            name="join",
            **params(len(shifts), x),
        )(*given)

    def whole(fresh_keys, fresh_values, turn_angle):
        rows = fresh_keys.shape[0] // n
        me = lax.axis_index(axes)
        lead = steps[0]
        first = lax.dynamic_slice_in_dim(fresh_keys, peer(me, lead) * rows, rows, 0)
        others = cut(fresh_keys, steps[1:], first)
        keys = [shift(b, d) for d, b in zip(steps, [first] + list(others))]
        cuts = cut(fresh_values, steps, others[0])
        values = [shift(b, d) for d, b in zip(steps, cuts)]
        moved_keys = join(fresh_keys, [0] + steps, [fresh_keys] + keys, None, first)
        turned_keys = rotate_pairs(moved_keys.astype(jnp.float32), turn_angle)
        key_scale = jnp.max(jnp.abs(turned_keys), axis=1)
        narrow_keys = (turned_keys / key_scale[:, None]).astype(jnp.bfloat16)
        ends = [n // 2, n - 4, n - 1]
        stored = join(fresh_values, [0] + steps[: ends[0]], [fresh_values] + values[: ends[0]], None, narrow_keys)
        for low, high in zip(ends, ends[1:]):
            stored = join(fresh_values, steps[low:high], values[low:high], stored, narrow_keys)
        return (narrow_keys, stored, key_scale)

    return jax.shard_map(
        whole,
        mesh=mesh,
        in_specs=(
            P(None, ("block", "span"), "heads", None),
            P(None, ("block", "span"), "heads", None),
            P(),
        ),
        out_specs=(
            P(("block", "span"), None, "heads", None),
            P(("block", "span"), None, "heads", None),
            P(("block", "span"), "heads", None),
        ),
        check_vma=False,
    )
```

time: 408 us -> 410 us (level)
  blocking collectives: 193 us -> 0 us
  starting transfers between devices: 4.75 us -> 168 us
  other arithmetic: 50 us -> 65 us
  local copies, waits for them, and re-layouts: 25.1 us -> 40 us
  Pallas kernels: 0 us -> 12.4 us
  waiting for transfers between devices: 134 us -> 124 us
    all_to_all x1 -> x0, blocking collectives: 193 us -> none  [local(): lax.all_to_all(fresh_keys, ('block', 'span'), split_axis=0, concat_axis=1...]
    ppermute x0 -> x30, starting transfers between devices: none -> 168 us  [shift(): return lax.ppermute(block, axes, [(i, peer(i, d)) for i in range(n)])]
    all_to_all x1 -> x0, waiting for transfers between devices: 134 us -> none  [local(): lax.all_to_all(fresh_values, ('block', 'span'), split_axis=0, concat_axis...]
    ppermute x0 -> x30, waiting for transfers between devices: none -> 124 us  [shift(): return lax.ppermute(block, axes, [(i, peer(i, d)) for i in range(n)])]
    sub x1, other arithmetic: 14.5 us -> 27.3 us  [rotate_pairs(): first * cosine - second * sine]
    pallas_call x0 -> x6, Pallas kernels: none -> 12.4 us  [the longest x4 8.75 us: join(): pl.pallas_call(kernel, out_shape=jax.ShapeDtypeStruct((rows, n * piece) +...]
    unnamed x11 -> x40, local copies, waits for them, and re-layouts: 9.08 us -> 21.3 us
    convert_element_type x2, other arithmetic: 16.2 us -> 22 us  [the longest x1 15.3 us: whole(): narrow_keys = (turned_keys / key_scale[:, None]).astype(jnp.bfloat16)]
  transfers between devices with their start and end apart: 1 -> 30, of which waited for: 1 -> 6; matrix products, arithmetic and copies ran while one was open for 16% -> 20% of each run, Pallas kernels for 0% -> 2%
where the time goes in v1:
time: 410 us; the launch traced here: 409 us
  starting transfers between devices  168 us (41%)
  waiting for transfers between devices  124 us (30%)
  other arithmetic  65 us (16%)
  local copies, waits for them, and re-layouts  40 us (10%)
  Pallas kernels  12.4 us (3%)
    ppermute x30, starting transfers between devices, shift(): return lax.ppermute(block, axes, [(i, peer(i, d)) for i in range(n)])  168 us
    ppermute x30, waiting for transfers between devices, shift(): return lax.ppermute(block, axes, [(i, peer(i, d)) for i in range(n)])  124 us
    sub x1, other arithmetic, rotate_pairs(): first * cosine - second * sine  27.3 us
    unnamed x40, local copies, waits for them, and re-layouts  21.3 us
    reduce_max x1, other arithmetic, whole(): key_scale = jnp.max(jnp.abs(turned_keys), axis=1)  15.7 us
    convert_element_type x1, other arithmetic, whole(): narrow_keys = (turned_keys / key_scale[:, None]).astype(jnp.bfloat16)  15.3 us
    cos x2, local copies, waits for them, and re-layouts, rotate_pairs(): jnp.cos(angle)[None, :, None, :]  13.6 us
    pallas_call x4, Pallas kernels, join(): pl.pallas_call(kernel, out_shape=jax.ShapeDtypeStruct((rows, n * piece) +...  8.75 us
  transfers between devices with their start and end apart: 30, of which 6 were waited for; matrix products, arithmetic and copies ran while one was open for 20% of the time, Pallas kernels for 2%

profile of v1, /device:TPU:0, one launch (start us, length us, event | category | flops | bytes accessed | tf_op | source)
XLA Modules:
  0.0 409.5 jit_solution(10389777383730401879)
XLA Ops:
  0.6 1.2 constant_dynamic-slice_fusion.after_ref.refs_16_
  1.9 3.4 copy-done.1
  5.3 2.3 cut.2
  7.6 6.0 %collective-permute-start.1 = (bf16[1,512,4,128]{3,2,1,0:T(4,128)(2,1)S(1)}, bf16[1,512,4,128]{3,2,1,0:T(4,128)(2,1)S(1)}, u32[]{:S(2)}, u32[]{:S(2)}) collective-permute-start(bf16[1,512,4,128]{3,2,1,0:T(4,128)(2,1)S(1)} %get-tuple-element.32.after_ref), channel_id=1, source_target_pairs={{0,28},{2,30},{4,0},{6,2},{8,4},{10,6},{12,8},{14,10},{16,12},{18,... | collective-permute-start | bytes 1572872 | tf_op jit(solution)/shard_map/ppermute | solution.py:79
  14.4 1.5 collective-permute-start.10
  15.9 1.5 collective-permute-start.11
  17.4 1.3 collective-permute-start.12
  18.7 1.0 collective-permute-start.13
  19.8 27.2 %collective-permute-done.1.refs_2_ = bf16[1,512,4,128]{3,2,1,0:T(4,128)(2,1)S(1)} collective-permute-done((bf16[1,512,4,128]{3,2,1,0:T(4,128)(2,1)S(1)}, bf16[1,512,4,128]{3,2,1,0:T(4,128)(2,1)S(1)}, u32[]{:S(2)}, u32[]{:S(2)}) %collective-permute-start.1) | collective-permute-done | bytes 524320 | tf_op jit(solution)/shard_map/ppermute | solution.py:79
  47.0 23.3 %collective-permute-start.2 = (bf16[1,512,4,128]{3,2,1,0:T(4,128)(2,1)S(1)}, bf16[1,512,4,128]{3,2,1,0:T(4,128)(2,1)S(1)}, u32[]{:S(2)}, u32[]{:S(2)}) collective-permute-start(bf16[1,512,4,128]{3,2,1,0:T(4,128)(2,1)S(1)} %get-tuple-element.33), channel_id=1, source_target_pairs={{0,10},{2,12},{4,14},{6,16},{8,18},{10,20},{12,22},{14,24},{16,26}... | collective-permute-start | bytes 1572872 | tf_op jit(solution)/shard_map/ppermute | solution.py:79
  70.3 3.3 collective-permute-start.3
  73.7 32.9 %collective-permute-done.13.refs_14_ = bf16[1,512,4,128]{3,2,1,0:T(4,128)(2,1)S(1)} collective-permute-done((bf16[1,512,4,128]{3,2,1,0:T(4,128)(2,1)S(1)}, bf16[1,512,4,128]{3,2,1,0:T(4,128)(2,1)S(1)}, u32[]{:S(2)}, u32[]{:S(2)}) %collective-permute-start.13) | collective-permute-done | bytes 524320 | tf_op jit(solution)/shard_map/ppermute | solution.py:79
  106.6 11.7 %collective-permute-start.5 = (bf16[1,512,4,128]{3,2,1,0:T(4,128)(2,1)S(1)}, bf16[1,512,4,128]{3,2,1,0:T(4,128)(2,1)S(1)}, u32[]{:S(2)}, u32[]{:S(2)}) collective-permute-start(bf16[1,512,4,128]{3,2,1,0:T(4,128)(2,1)S(1)} %get-tuple-element.36), channel_id=1, source_target_pairs={{0,20},{2,22},{4,24},{6,26},{8,28},{10,30},{12,0},{14,2},{16,4},{1... | collective-permute-start | bytes 1572872 | tf_op jit(solution)/shard_map/ppermute | solution.py:79
  120.0 14.4 %collective-permute-start.6 = (bf16[1,512,4,128]{3,2,1,0:T(4,128)(2,1)}, bf16[1,512,4,128]{3,2,1,0:T(4,128)(2,1)}, u32[]{:S(2)}, u32[]{:S(2)}) collective-permute-start(bf16[1,512,4,128]{3,2,1,0:T(4,128)(2,1)} %get-tuple-element.37), channel_id=1, source_target_pairs={{0,2},{2,4},{4,6},{6,8},{8,10},{10,12},{12,14},{14,16},{16,18},{18... | collective-permute-start | bytes 1572872 | tf_op jit(solution)/shard_map/ppermute | solution.py:79
  136.1 15.0 %collective-permute-done.5.refs_6_ = bf16[1,512,4,128]{3,2,1,0:T(4,128)(2,1)S(1)} collective-permute-done((bf16[1,512,4,128]{3,2,1,0:T(4,128)(2,1)S(1)}, bf16[1,512,4,128]{3,2,1,0:T(4,128)(2,1)S(1)}, u32[]{:S(2)}, u32[]{:S(2)}) %collective-permute-start.5) | collective-permute-done | bytes 524320 | tf_op jit(solution)/shard_map/ppermute | solution.py:79
  151.9 5.3 %collective-permute-start.9 = (bf16[1,512,4,128]{3,2,1,0:T(4,128)(2,1)}, bf16[1,512,4,128]{3,2,1,0:T(4,128)(2,1)}, u32[]{:S(2)}, u32[]{:S(2)}) collective-permute-start(bf16[1,512,4,128]{3,2,1,0:T(4,128)(2,1)} %get-tuple-element.40), channel_id=1, source_target_pairs={{0,12},{2,14},{4,16},{6,18},{8,20},{10,22},{12,24},{14,26},{16,28}... | collective-permute-start | bytes 1572872 | tf_op jit(solution)/shard_map/ppermute | solution.py:79
  157.2 9.7 %fusion = (f32[8192,64]{0,1:T(8,128)}, f32[8192,64]{0,1:T(8,128)}) fusion(f32[8192,64]{0,1:T(8,128)} %param.5), kind=kLoop, calls=%fused_computation.6 | loop fusion | bytes 6291456 | tf_op jit(solution)/shard_map/cos | solution.py:16
  166.9 3.8 copy.8
  170.8 3.8 copy.9
  174.6 3.4 copy-done.3
  178.0 1.0 copy-done.11
  179.0 1.4 cut.3
  180.4 9.6 %collective-permute-start.22 = (bf16[1,512,4,128]{3,2,1,0:T(4,128)(2,1)S(1)}, bf16[1,512,4,128]{3,2,1,0:T(4,128)(2,1)S(1)}, u32[]{:S(2)}, u32[]{:S(2)}) collective-permute-start(bf16[1,512,4,128]{3,2,1,0:T(4,128)(2,1)S(1)} %get-tuple-element.53), channel_id=1, source_target_pairs={{0,14},{2,16},{4,18},{6,20},{8,22},{10,24},{12,26},{14,28},{16,30}... | collective-permute-start | bytes 1572872 | tf_op jit(solution)/shard_map/ppermute | solution.py:79
  190.0 31.3 %collective-permute-start.23 = (bf16[1,512,4,128]{3,2,1,0:T(4,128)(2,1)S(1)}, bf16[1,512,4,128]{3,2,1,0:T(4,128)(2,1)S(1)}, u32[]{:S(2)}, u32[]{:S(2)}) collective-permute-start(bf16[1,512,4,128]{3,2,1,0:T(4,128)(2,1)S(1)} %get-tuple-element.54), channel_id=1, source_target_pairs={{0,28},{2,30},{4,0},{6,2},{8,4},{10,6},{12,8},{14,10},{16,12},{18,... | collective-permute-start | bytes 1572872 | tf_op jit(solution)/shard_map/ppermute | solution.py:79
  221.4 12.1 %collective-permute-start.26 = (bf16[1,512,4,128]{3,2,1,0:T(4,128)(2,1)S(1)}, bf16[1,512,4,128]{3,2,1,0:T(4,128)(2,1)S(1)}, u32[]{:S(2)}, u32[]{:S(2)}) collective-permute-start(bf16[1,512,4,128]{3,2,1,0:T(4,128)(2,1)S(1)} %get-tuple-element.57), channel_id=1, source_target_pairs={{0,6},{2,8},{4,10},{6,12},{8,14},{10,16},{12,18},{14,20},{16,22},{... | collective-permute-start | bytes 1572872 | tf_op jit(solution)/shard_map/ppermute | solution.py:79
  233.5 3.4 copy-done.2
  236.9 1.0 copy-done.5
  238.0 1.0 copy-done.7
  239.0 1.0 copy-done.9
  240.0 1.0 copy-done.13
  241.1 1.0 copy-done.15
  242.1 2.3 join.4
  244.5 6.6 %convert_element_type.6 = f32[1,8192,4,128]{3,2,1,0:T(4,128)} convert(bf16[1,8192,4,128]{3,2,1,0:T(4,128)(2,1)S(1)} %join.4) | non-fusion elementwise | flops 4194304 | bytes 25165824 | tf_op jit(solution)/shard_map/convert_element_type | solution.py:115
  251.1 27.3 %multiply_subtract_fusion = (f32[1,8192,4,64]{3,2,1,0:T(4,128)}, f32[1,8192,4,64]{3,2,1,0:T(4,128)}) fusion(f32[1,8192,4,128]{3,2,1,0:T(4,128)} %convert_element_type.6, f32[8192,64]{1,0:T(8,128)} %copy.9, f32[8192,64]{1,0:T(8,128)S(1)} %copy-done.16), kind=kLoop, calls=%fused_computation.3 | loop fusion | flops 12582912 | bytes 37748736 | tf_op jit(solution)/shard_map/sub | solution.py:19
  278.4 4.8 %collective-permute-start.28 = (bf16[1,512,4,128]{3,2,1,0:T(4,128)(2,1)S(1)}, bf16[1,512,4,128]{3,2,1,0:T(4,128)(2,1)S(1)}, u32[]{:S(2)}, u32[]{:S(2)}) collective-permute-start(bf16[1,512,4,128]{3,2,1,0:T(4,128)(2,1)S(1)} %get-tuple-element.59), channel_id=1, source_target_pairs={{0,2},{2,4},{4,6},{6,8},{8,10},{10,12},{12,14},{14,16},{16,18},{18... | collective-permute-start | bytes 1572872 | tf_op jit(solution)/shard_map/ppermute | solution.py:79
  283.4 5.5 %collective-permute-start.18 = (bf16[1,512,4,128]{3,2,1,0:T(4,128)(2,1)S(1)}, bf16[1,512,4,128]{3,2,1,0:T(4,128)(2,1)S(1)}, u32[]{:S(2)}, u32[]{:S(2)}) collective-permute-start(bf16[1,512,4,128]{3,2,1,0:T(4,128)(2,1)S(1)} %get-tuple-element.49), channel_id=1, source_target_pairs={{0,30},{2,0},{4,2},{6,4},{8,6},{10,8},{12,10},{14,12},{16,14},{18,... | collective-permute-start | bytes 1572872 | tf_op jit(solution)/shard_map/ppermute | solution.py:79
  289.1 15.7 %abs_reduce_fusion = f32[4,128]{1,0:T(4,128)S(1)} fusion(f32[1,8192,4,64]{3,2,1,0:T(4,128)} %get-tuple-element.62, f32[1,8192,4,64]{3,2,1,0:T(4,128)} %get-tuple-element.61), kind=kLoop, calls=%fused_computation.1 | loop fusion | flops 12582400 | bytes 16779264 | tf_op jit(solution)/shard_map/reduce_max | solution.py:116
  304.8 10.4 %collective-permute-done.27.refs_6_ = bf16[1,512,4,128]{3,2,1,0:T(4,128)(2,1)S(1)} collective-permute-done((bf16[1,512,4,128]{3,2,1,0:T(4,128)(2,1)S(1)}, bf16[1,512,4,128]{3,2,1,0:T(4,128)(2,1)S(1)}, u32[]{:S(2)}, u32[]{:S(2)}) %collective-permute-start.27) | collective-permute-done | bytes 524320 | tf_op jit(solution)/shard_map/ppermute | solution.py:79
  315.3 4.3 %collective-permute-start.21 = (bf16[1,512,4,128]{3,2,1,0:T(4,128)(2,1)S(1)}, bf16[1,512,4,128]{3,2,1,0:T(4,128)(2,1)S(1)}, u32[]{:S(2)}, u32[]{:S(2)}) collective-permute-start(bf16[1,512,4,128]{3,2,1,0:T(4,128)(2,1)S(1)} %get-tuple-element.52), channel_id=1, source_target_pairs={{0,8},{2,10},{4,12},{6,14},{8,16},{10,18},{12,20},{14,22},{16,24},... | collective-permute-start | bytes 1572872 | tf_op jit(solution)/shard_map/ppermute | solution.py:79
  319.5 3.9 collective-permute-start.15
  323.4 22.8 %collective-permute-start.16 = (bf16[1,512,4,128]{3,2,1,0:T(4,128)(2,1)S(1)}, bf16[1,512,4,128]{3,2,1,0:T(4,128)(2,1)S(1)}, u32[]{:S(2)}, u32[]{:S(2)}) collective-permute-start(bf16[1,512,4,128]{3,2,1,0:T(4,128)(2,1)S(1)} %get-tuple-element.47), channel_id=1, source_target_pairs={{0,4},{2,6},{4,8},{6,10},{8,12},{10,14},{12,16},{14,18},{16,20},{1... | collective-permute-start | bytes 1572872 | tf_op jit(solution)/shard_map/ppermute | solution.py:79
  346.2 27.2 %collective-permute-done.19.refs_1_ = bf16[1,512,4,128]{3,2,1,0:T(4,128)(2,1)S(1)} collective-permute-done((bf16[1,512,4,128]{3,2,1,0:T(4,128)(2,1)S(1)}, bf16[1,512,4,128]{3,2,1,0:T(4,128)(2,1)S(1)}, u32[]{:S(2)}, u32[]{:S(2)}) %collective-permute-start.19) | collective-permute-done | bytes 524320 | tf_op jit(solution)/shard_map/ppermute | solution.py:79
  373.4 3.4 collective-permute-start.17
  376.8 15.3 %divide_convert_fusion.refs_9_.refs_4_.refs_3_ = bf16[1,8192,4,128]{3,2,1,0:T(4,128)(2,1)S(1)} fusion(f32[4,128]{1,0:T(4,128)S(1)} %abs_reduce_fusion, f32[1,8192,4,64]{3,2,1,0:T(4,128)} %get-tuple-element.62, f32[1,8192,4,64]{3,2,1,0:T(4,128)} %get-tuple-element.61), kind=kLoop, calls=%fused_computation.4 | loop fusion | flops 12582912 | bytes 25167872 | tf_op jit(solution)/shard_map/convert_element_type | solution.py:117
  392.2 2.9 join.5.refs_5_
  395.1 2.2 join.6.refs_4_
  397.4 10.8 %collective-permute-done.16.refs_1_ = bf16[1,512,4,128]{3,2,1,0:T(4,128)(2,1)S(1)} collective-permute-done((bf16[1,512,4,128]{3,2,1,0:T(4,128)(2,1)S(1)}, bf16[1,512,4,128]{3,2,1,0:T(4,128)(2,1)S(1)}, u32[]{:S(2)}, u32[]{:S(2)}) %collective-permute-start.16) | collective-permute-done | bytes 524320 | tf_op jit(solution)/shard_map/ppermute | solution.py:79
  408.2 1.3 join.7
  (67 shorter events, 5.4 us)
Async XLA Ops:
  1.9 3.4 copy-start.1
  7.6 39.4 %collective-permute-start.1 = (bf16[1,512,4,128]{3,2,1,0:T(4,128)(2,1)S(1)}, bf16[1,512,4,128]{3,2,1,0:T(4,128)(2,1)S(1)}, u32[]{:S(2)}, u32[]{:S(2)}) collective-permute-start(bf16[1,512,4,128]{3,2,1,0:T(4,128)(2,1)S(1)} %get-tuple-element.32.after_ref), channel_id=1, source_target_pairs={{0,28},{2,30},{4,0},{6,2},{8,4},{10,6},{12,8},{14,10},{16,12},{18,... | collective-permute-start | bytes 1572872 | tf_op jit(solution)/shard_map/ppermute | solution.py:79
  13.6 0.8 copy-start.10
  14.4 32.6 %collective-permute-start.10 = (bf16[1,512,4,128]{3,2,1,0:T(4,128)(2,1)S(1)}, bf16[1,512,4,128]{3,2,1,0:T(4,128)(2,1)S(1)}, u32[]{:S(2)}, u32[]{:S(2)}) collective-permute-start(bf16[1,512,4,128]{3,2,1,0:T(4,128)(2,1)S(1)} %get-tuple-element.41), channel_id=1, source_target_pairs={{0,26},{2,28},{4,30},{6,0},{8,2},{10,4},{12,6},{14,8},{16,10},{18,... | collective-permute-start | bytes 1572872 | tf_op jit(solution)/shard_map/ppermute | solution.py:79
  15.9 54.4 %collective-permute-start.11 = (bf16[1,512,4,128]{3,2,1,0:T(4,128)(2,1)S(1)}, bf16[1,512,4,128]{3,2,1,0:T(4,128)(2,1)S(1)}, u32[]{:S(2)}, u32[]{:S(2)}) collective-permute-start(bf16[1,512,4,128]{3,2,1,0:T(4,128)(2,1)S(1)} %get-tuple-element.42), channel_id=1, source_target_pairs={{0,8},{2,10},{4,12},{6,14},{8,16},{10,18},{12,20},{14,22},{16,24},... | collective-permute-start | bytes 1572872 | tf_op jit(solution)/shard_map/ppermute | solution.py:79
  17.4 56.2 %collective-permute-start.12 = (bf16[1,512,4,128]{3,2,1,0:T(4,128)(2,1)S(1)}, bf16[1,512,4,128]{3,2,1,0:T(4,128)(2,1)S(1)}, u32[]{:S(2)}, u32[]{:S(2)}) collective-permute-start(bf16[1,512,4,128]{3,2,1,0:T(4,128)(2,1)S(1)} %get-tuple-element.43), channel_id=1, source_target_pairs={{0,22},{2,24},{4,26},{6,28},{8,30},{10,0},{12,2},{14,4},{16,6},{18... | collective-permute-start | bytes 1572872 | tf_op jit(solution)/shard_map/ppermute | solution.py:79
  18.7 87.9 %collective-permute-start.13 = (bf16[1,512,4,128]{3,2,1,0:T(4,128)(2,1)S(1)}, bf16[1,512,4,128]{3,2,1,0:T(4,128)(2,1)S(1)}, u32[]{:S(2)}, u32[]{:S(2)}) collective-permute-start(bf16[1,512,4,128]{3,2,1,0:T(4,128)(2,1)S(1)} %get-tuple-element.44), channel_id=1, source_target_pairs={{0,4},{2,6},{4,8},{6,10},{8,12},{10,14},{12,16},{14,18},{16,20},{1... | collective-permute-start | bytes 1572872 | tf_op jit(solution)/shard_map/ppermute | solution.py:79
  47.0 71.3 %collective-permute-start.14 = (bf16[1,512,4,128]{3,2,1,0:T(4,128)(2,1)S(1)}, bf16[1,512,4,128]{3,2,1,0:T(4,128)(2,1)S(1)}, u32[]{:S(2)}, u32[]{:S(2)}) collective-permute-start(bf16[1,512,4,128]{3,2,1,0:T(4,128)(2,1)S(1)} %get-tuple-element.45), channel_id=1, source_target_pairs={{0,18},{2,20},{4,22},{6,24},{8,26},{10,28},{12,30},{14,0},{16,2},{... | collective-permute-start | bytes 1572872 | tf_op jit(solution)/shard_map/ppermute | solution.py:79
  47.0 72.1 %collective-permute-start.2 = (bf16[1,512,4,128]{3,2,1,0:T(4,128)(2,1)S(1)}, bf16[1,512,4,128]{3,2,1,0:T(4,128)(2,1)S(1)}, u32[]{:S(2)}, u32[]{:S(2)}) collective-permute-start(bf16[1,512,4,128]{3,2,1,0:T(4,128)(2,1)S(1)} %get-tuple-element.33), channel_id=1, source_target_pairs={{0,10},{2,12},{4,14},{6,16},{8,18},{10,20},{12,22},{14,24},{16,26}... | collective-permute-start | bytes 1572872 | tf_op jit(solution)/shard_map/ppermute | solution.py:79
  70.3 64.1 %collective-permute-start.3 = (bf16[1,512,4,128]{3,2,1,0:T(4,128)(2,1)S(1)}, bf16[1,512,4,128]{3,2,1,0:T(4,128)(2,1)S(1)}, u32[]{:S(2)}, u32[]{:S(2)}) collective-permute-start(bf16[1,512,4,128]{3,2,1,0:T(4,128)(2,1)S(1)} %get-tuple-element.34), channel_id=1, source_target_pairs={{0,24},{2,26},{4,28},{6,30},{8,0},{10,2},{12,4},{14,6},{16,8},{18,... | collective-permute-start | bytes 1572872 | tf_op jit(solution)/shard_map/ppermute | solution.py:79
  73.7 61.6 %collective-permute-start.4 = (bf16[1,512,4,128]{3,2,1,0:T(4,128)(2,1)S(1)}, bf16[1,512,4,128]{3,2,1,0:T(4,128)(2,1)S(1)}, u32[]{:S(2)}, u32[]{:S(2)}) collective-permute-start(bf16[1,512,4,128]{3,2,1,0:T(4,128)(2,1)S(1)} %get-tuple-element.35), channel_id=1, source_target_pairs={{0,6},{2,8},{4,10},{6,12},{8,14},{10,16},{12,18},{14,20},{16,22},{... | collective-permute-start | bytes 1572872 | tf_op jit(solution)/shard_map/ppermute | solution.py:79
  106.6 44.5 %collective-permute-start.5 = (bf16[1,512,4,128]{3,2,1,0:T(4,128)(2,1)S(1)}, bf16[1,512,4,128]{3,2,1,0:T(4,128)(2,1)S(1)}, u32[]{:S(2)}, u32[]{:S(2)}) collective-permute-start(bf16[1,512,4,128]{3,2,1,0:T(4,128)(2,1)S(1)} %get-tuple-element.36), channel_id=1, source_target_pairs={{0,20},{2,22},{4,24},{6,26},{8,28},{10,30},{12,0},{14,2},{16,4},{1... | collective-permute-start | bytes 1572872 | tf_op jit(solution)/shard_map/ppermute | solution.py:79
  119.1 102.3 %collective-permute-start = (bf16[1,512,4,128]{3,2,1,0:T(4,128)(2,1)S(1)}, bf16[1,512,4,128]{3,2,1,0:T(4,128)(2,1)}, u32[]{:S(2)}, u32[]{:S(2)}) collective-permute-start(bf16[1,512,4,128]{3,2,1,0:T(4,128)(2,1)S(1)} %constant_dynamic-slice_fusion.after_ref.refs_16_), channel_id=1, source_target_pairs={{0,14},{2,16},{4,18},{6,20},{8,22},{10,24},{12,26},{14,28},{16,30}... | collective-permute-start | bytes 1572872 | tf_op jit(solution)/shard_map/ppermute | solution.py:79
  119.1 0.8 copy-start.6
  120.0 60.5 %collective-permute-start.6 = (bf16[1,512,4,128]{3,2,1,0:T(4,128)(2,1)}, bf16[1,512,4,128]{3,2,1,0:T(4,128)(2,1)}, u32[]{:S(2)}, u32[]{:S(2)}) collective-permute-start(bf16[1,512,4,128]{3,2,1,0:T(4,128)(2,1)} %get-tuple-element.37), channel_id=1, source_target_pairs={{0,2},{2,4},{4,6},{6,8},{8,10},{10,12},{12,14},{14,16},{16,18},{18... | collective-permute-start | bytes 1572872 | tf_op jit(solution)/shard_map/ppermute | solution.py:79
  134.4 0.9 copy-start.8
  135.3 54.7 %collective-permute-start.7 = (bf16[1,512,4,128]{3,2,1,0:T(4,128)(2,1)}, bf16[1,512,4,128]{3,2,1,0:T(4,128)(2,1)}, u32[]{:S(2)}, u32[]{:S(2)}) collective-permute-start(bf16[1,512,4,128]{3,2,1,0:T(4,128)(2,1)} %get-tuple-element.38), channel_id=1, source_target_pairs={{0,16},{2,18},{4,20},{6,22},{8,24},{10,26},{12,28},{14,30},{16,0},... | collective-permute-start | bytes 1572872 | tf_op jit(solution)/shard_map/ppermute | solution.py:79
  135.3 0.8 copy-start.12
  136.1 85.2 %collective-permute-start.8 = (bf16[1,512,4,128]{3,2,1,0:T(4,128)(2,1)}, bf16[1,512,4,128]{3,2,1,0:T(4,128)(2,1)}, u32[]{:S(2)}, u32[]{:S(2)}) collective-permute-start(bf16[1,512,4,128]{3,2,1,0:T(4,128)(2,1)} %get-tuple-element.39), channel_id=1, source_target_pairs={{0,30},{2,0},{4,2},{6,4},{8,6},{10,8},{12,10},{14,12},{16,14},{18,... | collective-permute-start | bytes 1572872 | tf_op jit(solution)/shard_map/ppermute | solution.py:79
  151.9 69.4 %collective-permute-start.9 = (bf16[1,512,4,128]{3,2,1,0:T(4,128)(2,1)}, bf16[1,512,4,128]{3,2,1,0:T(4,128)(2,1)}, u32[]{:S(2)}, u32[]{:S(2)}) collective-permute-start(bf16[1,512,4,128]{3,2,1,0:T(4,128)(2,1)} %get-tuple-element.40), channel_id=1, source_target_pairs={{0,12},{2,14},{4,16},{6,18},{8,20},{10,22},{12,24},{14,26},{16,28}... | collective-permute-start | bytes 1572872 | tf_op jit(solution)/shard_map/ppermute | solution.py:79
  174.6 3.4 copy-start.3
  178.0 1.0 copy-start.11
  180.4 98.0 %collective-permute-start.22 = (bf16[1,512,4,128]{3,2,1,0:T(4,128)(2,1)S(1)}, bf16[1,512,4,128]{3,2,1,0:T(4,128)(2,1)S(1)}, u32[]{:S(2)}, u32[]{:S(2)}) collective-permute-start(bf16[1,512,4,128]{3,2,1,0:T(4,128)(2,1)S(1)} %get-tuple-element.53), channel_id=1, source_target_pairs={{0,14},{2,16},{4,18},{6,20},{8,22},{10,24},{12,26},{14,28},{16,30}... | collective-permute-start | bytes 1572872 | tf_op jit(solution)/shard_map/ppermute | solution.py:79
  190.0 88.4 %collective-permute-start.23 = (bf16[1,512,4,128]{3,2,1,0:T(4,128)(2,1)S(1)}, bf16[1,512,4,128]{3,2,1,0:T(4,128)(2,1)S(1)}, u32[]{:S(2)}, u32[]{:S(2)}) collective-permute-start(bf16[1,512,4,128]{3,2,1,0:T(4,128)(2,1)S(1)} %get-tuple-element.54), channel_id=1, source_target_pairs={{0,28},{2,30},{4,0},{6,2},{8,4},{10,6},{12,8},{14,10},{16,12},{18,... | collective-permute-start | bytes 1572872 | tf_op jit(solution)/shard_map/ppermute | solution.py:79
  221.3 61.9 %collective-permute-start.24 = (bf16[1,512,4,128]{3,2,1,0:T(4,128)(2,1)S(1)}, bf16[1,512,4,128]{3,2,1,0:T(4,128)(2,1)S(1)}, u32[]{:S(2)}, u32[]{:S(2)}) collective-permute-start(bf16[1,512,4,128]{3,2,1,0:T(4,128)(2,1)S(1)} %get-tuple-element.55), channel_id=1, source_target_pairs={{0,10},{2,12},{4,14},{6,16},{8,18},{10,20},{12,22},{14,24},{16,26}... | collective-permute-start | bytes 1572872 | tf_op jit(solution)/shard_map/ppermute | solution.py:79
  221.3 62.1 %collective-permute-start.25 = (bf16[1,512,4,128]{3,2,1,0:T(4,128)(2,1)S(1)}, bf16[1,512,4,128]{3,2,1,0:T(4,128)(2,1)S(1)}, u32[]{:S(2)}, u32[]{:S(2)}) collective-permute-start(bf16[1,512,4,128]{3,2,1,0:T(4,128)(2,1)S(1)} %get-tuple-element.56), channel_id=1, source_target_pairs={{0,24},{2,26},{4,28},{6,30},{8,0},{10,2},{12,4},{14,6},{16,8},{18,... | collective-permute-start | bytes 1572872 | tf_op jit(solution)/shard_map/ppermute | solution.py:79
  221.4 67.5 %collective-permute-start.26 = (bf16[1,512,4,128]{3,2,1,0:T(4,128)(2,1)S(1)}, bf16[1,512,4,128]{3,2,1,0:T(4,128)(2,1)S(1)}, u32[]{:S(2)}, u32[]{:S(2)}) collective-permute-start(bf16[1,512,4,128]{3,2,1,0:T(4,128)(2,1)S(1)} %get-tuple-element.57), channel_id=1, source_target_pairs={{0,6},{2,8},{4,10},{6,12},{8,14},{10,16},{12,18},{14,20},{16,22},{... | collective-permute-start | bytes 1572872 | tf_op jit(solution)/shard_map/ppermute | solution.py:79
  233.5 3.4 copy-start.2
  236.9 1.0 copy-start.5
  238.0 1.0 copy-start.7
  239.0 1.0 copy-start.9
  240.0 1.0 copy-start.13
  241.1 1.0 copy-start.15
  244.4 6.6 %copy-start.16 = (f32[8192,64]{1,0:T(8,128)S(1)}, f32[8192,64]{1,0:T(8,128)}, u32[]{:S(2)}) copy-start(f32[8192,64]{1,0:T(8,128)} %copy.8) | copy-start | bytes 6291460
  278.4 36.9 %collective-permute-start.27 = (bf16[1,512,4,128]{3,2,1,0:T(4,128)(2,1)S(1)}, bf16[1,512,4,128]{3,2,1,0:T(4,128)(2,1)S(1)}, u32[]{:S(2)}, u32[]{:S(2)}) collective-permute-start(bf16[1,512,4,128]{3,2,1,0:T(4,128)(2,1)S(1)} %get-tuple-element.58), channel_id=1, source_target_pairs={{0,20},{2,22},{4,24},{6,26},{8,28},{10,30},{12,0},{14,2},{16,4},{1... | collective-permute-start | bytes 1572872 | tf_op jit(solution)/shard_map/ppermute | solution.py:79
  278.4 36.8 %collective-permute-start.28 = (bf16[1,512,4,128]{3,2,1,0:T(4,128)(2,1)S(1)}, bf16[1,512,4,128]{3,2,1,0:T(4,128)(2,1)S(1)}, u32[]{:S(2)}, u32[]{:S(2)}) collective-permute-start(bf16[1,512,4,128]{3,2,1,0:T(4,128)(2,1)S(1)} %get-tuple-element.59), channel_id=1, source_target_pairs={{0,2},{2,4},{4,6},{6,8},{8,10},{10,12},{12,14},{14,16},{16,18},{18... | collective-permute-start | bytes 1572872 | tf_op jit(solution)/shard_map/ppermute | solution.py:79
  283.2 36.3 %collective-permute-start.29 = (bf16[1,512,4,128]{3,2,1,0:T(4,128)(2,1)S(1)}, bf16[1,512,4,128]{3,2,1,0:T(4,128)(2,1)S(1)}, u32[]{:S(2)}, u32[]{:S(2)}) collective-permute-start(bf16[1,512,4,128]{3,2,1,0:T(4,128)(2,1)S(1)} %get-tuple-element.60), channel_id=1, source_target_pairs={{0,16},{2,18},{4,20},{6,22},{8,24},{10,26},{12,28},{14,30},{16,0},... | collective-permute-start | bytes 1572872 | tf_op jit(solution)/shard_map/ppermute | solution.py:79
  283.4 40.0 %collective-permute-start.18 = (bf16[1,512,4,128]{3,2,1,0:T(4,128)(2,1)S(1)}, bf16[1,512,4,128]{3,2,1,0:T(4,128)(2,1)S(1)}, u32[]{:S(2)}, u32[]{:S(2)}) collective-permute-start(bf16[1,512,4,128]{3,2,1,0:T(4,128)(2,1)S(1)} %get-tuple-element.49), channel_id=1, source_target_pairs={{0,30},{2,0},{4,2},{6,4},{8,6},{10,8},{12,10},{14,12},{16,14},{18,... | collective-permute-start | bytes 1572872 | tf_op jit(solution)/shard_map/ppermute | solution.py:79
  288.9 84.5 %collective-permute-start.19 = (bf16[1,512,4,128]{3,2,1,0:T(4,128)(2,1)S(1)}, bf16[1,512,4,128]{3,2,1,0:T(4,128)(2,1)S(1)}, u32[]{:S(2)}, u32[]{:S(2)}) collective-permute-start(bf16[1,512,4,128]{3,2,1,0:T(4,128)(2,1)S(1)} %get-tuple-element.50), channel_id=1, source_target_pairs={{0,12},{2,14},{4,16},{6,18},{8,20},{10,22},{12,24},{14,26},{16,28}... | collective-permute-start | bytes 1572872 | tf_op jit(solution)/shard_map/ppermute | solution.py:79
  304.8 87.3 %copy-start.17 = (f32[4,128]{1,0:T(4,128)}, f32[4,128]{1,0:T(4,128)S(1)}, u32[]{:S(2)}) copy-start(f32[4,128]{1,0:T(4,128)S(1)} %abs_reduce_fusion) | copy-start | bytes 6148
  315.3 79.9 %collective-permute-start.20 = (bf16[1,512,4,128]{3,2,1,0:T(4,128)(2,1)S(1)}, bf16[1,512,4,128]{3,2,1,0:T(4,128)(2,1)S(1)}, u32[]{:S(2)}, u32[]{:S(2)}) collective-permute-start(bf16[1,512,4,128]{3,2,1,0:T(4,128)(2,1)S(1)} %get-tuple-element.51), channel_id=1, source_target_pairs={{0,26},{2,28},{4,30},{6,0},{8,2},{10,4},{12,6},{14,8},{16,10},{18,... | collective-permute-start | bytes 1572872 | tf_op jit(solution)/shard_map/ppermute | solution.py:79
  315.3 79.9 %collective-permute-start.21 = (bf16[1,512,4,128]{3,2,1,0:T(4,128)(2,1)S(1)}, bf16[1,512,4,128]{3,2,1,0:T(4,128)(2,1)S(1)}, u32[]{:S(2)}, u32[]{:S(2)}) collective-permute-start(bf16[1,512,4,128]{3,2,1,0:T(4,128)(2,1)S(1)} %get-tuple-element.52), channel_id=1, source_target_pairs={{0,8},{2,10},{4,12},{6,14},{8,16},{10,18},{12,20},{14,22},{16,24},... | collective-permute-start | bytes 1572872 | tf_op jit(solution)/shard_map/ppermute | solution.py:79
  319.5 77.9 %collective-permute-start.15 = (bf16[1,512,4,128]{3,2,1,0:T(4,128)(2,1)S(1)}, bf16[1,512,4,128]{3,2,1,0:T(4,128)(2,1)S(1)}, u32[]{:S(2)}, u32[]{:S(2)}) collective-permute-start(bf16[1,512,4,128]{3,2,1,0:T(4,128)(2,1)S(1)} %get-tuple-element.46), channel_id=1, source_target_pairs={{0,22},{2,24},{4,26},{6,28},{8,30},{10,0},{12,2},{14,4},{16,6},{18... | collective-permute-start | bytes 1572872 | tf_op jit(solution)/shard_map/ppermute | solution.py:79
  323.4 84.8 %collective-permute-start.16 = (bf16[1,512,4,128]{3,2,1,0:T(4,128)(2,1)S(1)}, bf16[1,512,4,128]{3,2,1,0:T(4,128)(2,1)S(1)}, u32[]{:S(2)}, u32[]{:S(2)}) collective-permute-start(bf16[1,512,4,128]{3,2,1,0:T(4,128)(2,1)S(1)} %get-tuple-element.47), channel_id=1, source_target_pairs={{0,4},{2,6},{4,8},{6,10},{8,12},{10,14},{12,16},{14,18},{16,20},{1... | collective-permute-start | bytes 1572872 | tf_op jit(solution)/shard_map/ppermute | solution.py:79
  373.4 18.7 %slice-start = ((s8[8388608]{0:T(1024)(128)(4,1)}), s8[4194304]{0:T(1024)(128)(4,1)S(1)}, s32[]{:S(2)}) async-start(s8[8388608]{0:T(1024)(128)(4,1)} %bitcast.1), calls=%async_computation | async-start | bytes 8388608
  373.4 18.8 %slice-start.1 = ((s8[8388608]{0:T(1024)(128)(4,1)}), s8[4194304]{0:T(1024)(128)(4,1)S(1)}, s32[]{:S(2)}) async-start(s8[8388608]{0:T(1024)(128)(4,1)} %bitcast.1), calls=%async_computation.1 | async-start | bytes 8388608
  373.4 34.7 %collective-permute-start.17 = (bf16[1,512,4,128]{3,2,1,0:T(4,128)(2,1)S(1)}, bf16[1,512,4,128]{3,2,1,0:T(4,128)(2,1)S(1)}, u32[]{:S(2)}, u32[]{:S(2)}) collective-permute-start(bf16[1,512,4,128]{3,2,1,0:T(4,128)(2,1)S(1)} %get-tuple-element.48), channel_id=1, source_target_pairs={{0,18},{2,20},{4,22},{6,24},{8,26},{10,28},{12,30},{14,0},{16,2},{... | collective-permute-start | bytes 1572872 | tf_op jit(solution)/shard_map/ppermute | solution.py:79
  392.2 16.0 %copy-start = (bf16[1,8192,4,128]{3,2,1,0:T(4,128)(2,1)}, bf16[1,8192,4,128]{3,2,1,0:T(4,128)(2,1)S(1)}, u32[]{:S(2)}) copy-start(bf16[1,8192,4,128]{3,2,1,0:T(4,128)(2,1)S(1)} %divide_convert_fusion.refs_9_.refs_4_.refs_3_) | copy-start | bytes 25165828
  (2 other events, 1.6 us)
